TPU v7x, 32 devices: a whole 2x2x4 slice. The times are simulated.
32 devices in a mesh: seq: 8 (over y, x, core), tensor: 4 (over z).
Axes of the slice: x: 2, y: 2, z: 4, core: 2. Of those that a mesh axis runs over, the one named last changes fastest.
Arguments:
- streams: float32 [4, 4096, 4096], P(None, 'seq', 'tensor'), may hold values from -8 to 8
- mix_weight: float32 [24, 4, 4096], P(None, None, 'tensor'), may hold values from -0.046875 to 0.046875
- mix_bias: float32 [24], replicated, may hold values from -4 to 4
- mix_scale: float32 [3], replicated, may hold values from 1 to 2
- norm_gain: bfloat16 [4096], replicated, may hold values from 0.25 to 1.75
- gate_weight: bfloat16 [4096, 7168], P('seq', 'tensor'), may hold values from -0.09375 to 0.09375
- up_weight: bfloat16 [4096, 7168], P('seq', 'tensor'), may hold values from -0.09375 to 0.09375
- down_weight: bfloat16 [7168, 4096], P('tensor', 'seq'), may hold values from -0.0625 to 0.0625
Outputs:
- new_streams: float32 [4, 4096, 4096], P(None, 'seq', 'tensor')
All inputs are finite; a program needn't handle non-finite values.
Results may differ from a plain program's by a relative error of at most 0.01.
Values may be sent and summed in bfloat16 or wider, within the bound.
A program may use at most 128 MiB of HBM per device.

v0:
```python
import jax
import jax.numpy as jnp
from jax import lax
from jax.sharding import PartitionSpec as P

D = 4096
STREAMS = 4
SWEEPS = 20
epsilon = 0.25


def coefficients(logits, mix_bias, mix_scale):
    pre_mix = jax.nn.sigmoid(mix_scale[0] * logits[:STREAMS] + mix_bias[:STREAMS, None])
    post_mix = 2.0 * jax.nn.sigmoid(
        mix_scale[1] * logits[STREAMS : 2 * STREAMS] + mix_bias[STREAMS : 2 * STREAMS, None]
    )
    start_mix = jnp.exp(mix_scale[2] * logits[2 * STREAMS :] + mix_bias[2 * STREAMS :, None])
    start_mix = start_mix.reshape(STREAMS, STREAMS, logits.shape[1])

    def balance(iteration, matrix):
        matrix = matrix / jnp.sum(matrix, axis=1, keepdims=True)
        return matrix / jnp.sum(matrix, axis=0, keepdims=True)

    return (pre_mix, post_mix, lax.fori_loop(0, SWEEPS, balance, start_mix))


def project_logits(mix_weight, values):
    return jnp.einsum("lkd,ktd->lt", mix_weight, values, precision=lax.Precision.HIGHEST)


def add_rows(normed, segment):
    return jnp.dot(normed, segment, preferred_element_type=jnp.float32)


def body(streams, mix_weight, mix_bias, mix_scale, norm_gain, gate_weight, up_weight, down_weight):
    feature_count = STREAMS * D
    squares = jnp.sum(streams * streams, axis=(0, 2))[None, :]
    raw_logits = project_logits(mix_weight, streams)
    totals, raw_sums = (
        lax.psum(squares.astype(jnp.bfloat16), "tensor").astype(jnp.float32),
        lax.psum(raw_logits.astype(jnp.bfloat16), "tensor").astype(jnp.float32),
    )
    logits = raw_sums * lax.rsqrt(totals / feature_count + epsilon)
    pre_mix, post_mix, res_mix = coefficients(logits, mix_bias, mix_scale)
    layer_in = jnp.sum(pre_mix[:, :, None] * streams, axis=0).astype(jnp.bfloat16)
    whole_input = lax.all_gather(layer_in, "tensor", axis=1, tiled=True)
    as_float = whole_input.astype(jnp.float32)
    mean_square = jnp.mean(as_float * as_float, axis=1, keepdims=True)
    normed = (as_float * lax.rsqrt(mean_square + epsilon) * norm_gain.astype(jnp.float32)).astype(
        jnp.bfloat16
    )

    def add_single(segment):
        return add_rows(normed, segment)

    gate_value = add_single(lax.all_gather(gate_weight, "seq", axis=0, tiled=True))
    up_value = add_single(lax.all_gather(up_weight, "seq", axis=0, tiled=True))
    hidden = (jax.nn.silu(gate_value) * up_value).astype(jnp.bfloat16)
    partial_out = jnp.dot(
        hidden,
        lax.all_gather(down_weight, "seq", axis=1, tiled=True),
        preferred_element_type=jnp.float32,
    )
    layer_out = lax.psum_scatter(
        partial_out.astype(jnp.bfloat16), "tensor", scatter_dimension=1, tiled=True
    ).astype(jnp.float32)
    outputs = []
    for target in range(STREAMS):
        mixed = post_mix[target][:, None] * layer_out
        for source in range(STREAMS):
            mixed = mixed + res_mix[target, source][:, None] * streams[source]
        outputs.append(mixed)
    return jnp.stack(outputs)


def solution(mesh):
    placed = (
        P(None, "seq", "tensor"),
        P(None, None, "tensor"),
        P(),
        P(),
        P(),
        P("seq", "tensor"),
        P("seq", "tensor"),
        P("tensor", "seq"),
    )
    return jax.shard_map(
        body, mesh=mesh, in_specs=placed, out_specs=P(None, "seq", "tensor"), check_vma=False
    )
```

profile of v0, /device:TPU:0, one launch (start us, length us, event | category | flops | bytes accessed | tf_op | source)
XLA Modules:
  0.0 502.4 jit_solution(2445068829800795499)
XLA Ops:
  6.5 4.2 multiply_reduce_fusion.1
  10.7 1.6 copy-done
  12.3 8.1 %fusion.28 = bf16[24,512]{1,0:T(8,128)(2,1)S(1)} fusion(f32[4,512,1024]{2,1,0:T(8,128)S(1)} %copy-done, f32[24,4,1024]{2,1,0:T(4,128)} %param.11), kind=kOutput, calls=%fused_computation.55 | convolution fusion | flops 603992064 | bytes 8806400 | tf_op jit(solution)/shard_map/lkd,ktd->lt/dot_general | solution.py:28
  20.5 20.8 %all-reduce = (bf16[24,512]{1,0:T(8,128)(2,1)S(1)}, bf16[1,512]{1,0:T(2,128)(2,1)S(1)}) all-reduce(bf16[24,512]{1,0:T(8,128)(2,1)S(1)} %fusion.28, bf16[1,512]{1,0:T(2,128)(2,1)S(1)} %convert_element_type.47), channel_id=1, replica_groups=mesh['seq'=8,'tensor'=4] {'tensor'}, use_global_device_ids=true, to_apply=%region_0.0 | all-reduce | flops 12800 | bytes 51200 | tf_op jit(solution)/shard_map/psum | solution.py:41
  41.3 0.7 fusion.46
  42.0 0.1 fusion.47
  42.0 1.4 fusion.42
  43.5 5.3 %multiply_reduce_fusion = bf16[512,1024]{1,0:T(8,128)(2,1)} fusion(f32[4,512,1024]{2,1,0:T(8,128)} %param.10, f32[4,512]{1,0:T(4,128)S(1)} %get-tuple-element.29), kind=kLoop, calls=%fused_computation.8 | loop fusion | flops 3670016 | bytes 9445376 | tf_op jit(solution)/shard_map/reduce_sum | solution.py:45
  48.7 0.0 all-gather.5.cloned.1.call-update
  48.7 0.0 all-gather.7.cloned.1.call-start
  48.8 0.7 all-gather.7.cloned.1.call-update
  49.5 0.0 copy-start.2
  49.5 0.0 all-gather.11.cloned.1.call-start
  49.5 0.7 all-gather.11.cloned.1.call-update
  50.2 0.0 all-gather.9.cloned.1.call-start
  50.3 0.5 all-gather.9.cloned.1.call-update
  50.8 0.0 reduce-scatter.2.cloned.1.call-start
  50.9 77.0 %all-gather.5.cloned.1.call-done = bf16[512,4096]{1,0:T(8,128)(2,1)} async-done(((bf16[512,1024]{1,0:T(8,128)(2,1)}), bf16[512,4096]{1,0:T(8,128)(2,1)}) %all-gather.5.cloned.1.call-update) | async-done | bytes 4194320 | tf_op jit(solution)/shard_map/all_gather | solution.py:46
  127.9 3.1 fusion
  131.0 78.2 %all-gather.7.cloned.1.call-done = bf16[4096,1792]{1,0:T(8,128)(2,1)} async-done(((bf16[512,1792]{1,0:T(8,128)(2,1)}), bf16[4096,1792]{1,0:T(8,128)(2,1)}) %all-gather.7.cloned.1.call-update) | async-done | bytes 14680080 | tf_op jit(solution)/shard_map/all_gather | solution.py:56
  209.1 14.7 %fusion.26 = f32[512,1792]{1,0:T(8,128)} fusion(bf16[4096,1792]{1,0:T(8,128)(2,1)} %all-gather.7.cloned.1.call-done, bf16[512,4096]{1,0:T(8,128)(2,1)} %all-gather.5.cloned.1.call-done, f32[4096]{0:T(1024)S(1)} %convert_element_type.51, f32[512]{0:T(512)S(1)} %add_rsqrt_fusion), kind=kOutput, calls=%fused_computation.53 | convolution fusion | flops 7524581376 | bytes 22562816 | tf_op jit(solution)/shard_map/dot_general | solution.py:32
  223.8 70.9 %all-gather.11.cloned.1.call-done = bf16[1792,4096]{1,0:T(8,128)(2,1)} async-done(((bf16[1792,512]{1,0:T(8,128)(2,1)}), bf16[1792,4096]{1,0:T(8,128)(2,1)}) %all-gather.11.cloned.1.call-update) | async-done | bytes 14680080 | tf_op jit(solution)/shard_map/all_gather | solution.py:61
  294.8 82.6 %all-gather.9.cloned.1.call-done = bf16[4096,1792]{1,0:T(8,128)(2,1)} async-done(((bf16[512,1792]{1,0:T(8,128)(2,1)}), bf16[4096,1792]{1,0:T(8,128)(2,1)}) %all-gather.9.cloned.1.call-update) | async-done | bytes 14680080 | tf_op jit(solution)/shard_map/all_gather | solution.py:57
  377.4 28.8 %convolution_convert_fusion = bf16[512,4096]{1,0:T(8,128)(2,1)} fusion(bf16[1792,4096]{1,0:T(8,128)(2,1)} %all-gather.11.cloned.1.call-done, f32[512,1792]{1,0:T(8,128)} %fusion.26, bf16[4096,1792]{1,0:T(8,128)(2,1)} %all-gather.9.cloned.1.call-done, bf16[512,4096]{1,0:T(8,128)(2,1)} %all-gather.5.cloned.1.call-done, f32[4096]{0:T(1024)S(1)} %convert_element_type.51, ...), kind=kOutput, calls=%fused_computation.10 | convolution fusion | flops 15048376320 | bytes 41437184 | tf_op jit(solution)/shard_map/dot_general | solution.py:59
  406.2 0.0 reduce-scatter.2.cloned.1.call-update
  406.2 0.1 slice.120
  406.3 0.8 fusion.31
  407.1 2.1 while.10
  409.3 73.9 %reduce-scatter.2.cloned.1.call-done = bf16[512,1024]{1,0:T(8,128)(2,1)} async-done(((bf16[512,4096]{1,0:T(8,128)(2,1)}), bf16[512,1024]{1,0:T(8,128)(2,1)}) %reduce-scatter.2.cloned.1.call-update) | async-done | bytes 1048592 | tf_op jit(solution)/shard_map/reduce_scatter | solution.py:64
  483.2 4.7 fusion.7
  487.8 4.3 fusion.17
  492.1 3.7 pad_maximum_fusion
  (77 shorter events, 1.8 us)
Async XLA Ops:
  6.5 121.3 %all-gather.5.cloned.1.call-start = ((), (), s32[]{:S(2)}) async-start(), calls=%async_computation.1 | async-start | bytes 5242880 | tf_op jit(solution)/shard_map/all_gather | solution.py:46
  6.5 5.8 %copy-start = (f32[4,512,1024]{2,1,0:T(8,128)S(1)}, f32[4,512,1024]{2,1,0:T(8,128)}, u32[]{:S(2)}) copy-start(f32[4,512,1024]{2,1,0:T(8,128)} %param.10) | copy-start | bytes 25165828
  12.3 29.0 %copy-start.3 = (f32[3]{0:T(128)S(1)}, f32[3]{0:T(128)}, u32[]{:S(2)}) copy-start(f32[3]{0:T(128)} %param.13) | copy-start | bytes 40
  12.3 29.7 %copy-start.4 = (f32[24]{0:T(128)S(1)}, f32[24]{0:T(128)}, u32[]{:S(2)}) copy-start(f32[24]{0:T(128)} %param.12) | copy-start | bytes 292
  48.7 160.4 %all-gather.7.cloned.1.call-start = ((), (), s32[]{:S(2)}) async-start(), calls=%async_computation.2 | async-start | bytes 16515072 | tf_op jit(solution)/shard_map/all_gather | solution.py:56
  49.5 1.4 copy-start.2
  49.5 245.3 %all-gather.11.cloned.1.call-start = ((), (), s32[]{:S(2)}) async-start(), calls=%async_computation.4 | async-start | bytes 16515072 | tf_op jit(solution)/shard_map/all_gather | solution.py:61
  50.2 327.2 %all-gather.9.cloned.1.call-start = ((), (), s32[]{:S(2)}) async-start(), calls=%async_computation.3 | async-start | bytes 16515072 | tf_op jit(solution)/shard_map/all_gather | solution.py:57
  50.8 432.3 %reduce-scatter.2.cloned.1.call-start = ((), (), s32[]{:S(2)}) async-start(), calls=%async_computation.5 | async-start | bytes 5242880 | tf_op jit(solution)/shard_map/reduce_scatter | solution.py:64
  483.2 4.7 copy-start.1
Sparse Core Ops, SparseCore 0:
  48.9 78.9 all-gather.4
  129.8 79.3 all-gather.6
  211.0 83.7 all-gather.10
  296.5 80.8 all-gather.8
  406.3 76.7 reduce-scatter.1
where the time goes:
time: 503 us; the launch traced here: 502 us
  waiting for transfers between devices  385 us (77%)
  matrix products  51.6 us (10%)
  other arithmetic  29.1 us (6%)
  blocking collectives  20.8 us (4%)
  between operations  13.3 us (3%)
    all_gather x1, waiting for transfers between devices, body(): up_value = add_single(lax.all_gather(up_weight, 'seq', axis=0, tiled=True))  82.6 us
    all_gather x1, waiting for transfers between devices, body(): lax.all_gather(gate_weight, 'seq', axis=0, tiled=True)  78.2 us
    all_gather x1, waiting for transfers between devices, body(): whole_input = lax.all_gather(layer_in, 'tensor', axis=1, tiled=True)  77 us
    reduce_scatter x1, waiting for transfers between devices, body(): lax.psum_scatter(partial_out.astype(jnp.bfloat16), 'tensor', scatter_dime...  73.9 us
    all_gather x1, waiting for transfers between devices, body(): lax.all_gather(down_weight, 'seq', axis=1, tiled=True)  70.9 us
    dot_general x1, matrix products, body(): jnp.dot(hidden, lax.all_gather(down_weight, 'seq', axis=1, tiled=True), p...  28.8 us
    psum x1, blocking collectives, body(): lax.psum(raw_logits.astype(jnp.bfloat16), 'tensor').astype(jnp.float32)  20.8 us
    dot_general x1, matrix products, add_rows(): return jnp.dot(normed, segment, preferred_element_type=jnp.float32)  14.7 us
  transfers between devices with their start and end apart: 5, of which 5 were waited for; matrix products, arithmetic and copies ran while one was open for 4% of the time, Pallas kernels for 0%

commit v1 on v0

--- a/solution.py
+++ b/solution.py
@@ -43,7 +43,14 @@
     logits = raw_sums * lax.rsqrt(totals / feature_count + epsilon)
     pre_mix, post_mix, res_mix = coefficients(logits, mix_bias, mix_scale)
     layer_in = jnp.sum(pre_mix[:, :, None] * streams, axis=0).astype(jnp.bfloat16)
-    whole_input = lax.all_gather(layer_in, "tensor", axis=1, tiled=True)
+    ring = [layer_in]
+    for hop in range(3):
+        ring.append(lax.ppermute(ring[-1], "tensor", [(dev, (dev + 1) % 4) for dev in range(4)]))
+    whole_input = jnp.roll(
+        jnp.concatenate(ring[::-1], axis=1),
+        (lax.axis_index("tensor") + 1) * ring[0].shape[1],
+        axis=1,
+    )
     as_float = whole_input.astype(jnp.float32)
     mean_square = jnp.mean(as_float * as_float, axis=1, keepdims=True)
     normed = (as_float * lax.rsqrt(mean_square + epsilon) * norm_gain.astype(jnp.float32)).astype(

time: 503 us -> 386 us (0.77)
  waiting for transfers between devices: 385 us -> 265 us
  local copies, waits for them, and re-layouts: 2.49 us -> 11.4 us
  other arithmetic: 29.1 us -> 23.7 us
    all_gather x1, waiting for transfers between devices: 78.2 us -> 0.02 us  [body(): lax.all_gather(gate_weight, 'seq', axis=0, tiled=True)]
    all_gather x1 -> x0, waiting for transfers between devices: 77 us -> none  [body(): whole_input = lax.all_gather(layer_in, 'tensor', axis=1, tiled=True)]
    ppermute x0 -> x3, waiting for transfers between devices: none -> 67.9 us  [body(): lax.ppermute(ring[-1], 'tensor', [(dev, (dev + 1) % 4) for dev in range(4)])]
    all_gather x1, waiting for transfers between devices: 82.6 us -> 35.8 us  [body(): up_value = add_single(lax.all_gather(up_weight, 'seq', axis=0, tiled=True))]
    all_gather x1, waiting for transfers between devices: 70.9 us -> 85.6 us  [body(): lax.all_gather(down_weight, 'seq', axis=1, tiled=True)]
    unnamed x10 -> x31, local copies, waits for them, and re-layouts: 1.62 us -> 10.4 us
  transfers between devices with their start and end apart: 5 -> 7, of which waited for: 5 -> 6; matrix products, arithmetic and copies ran while one was open for 4% -> 10% of each run, Pallas kernels for 0% -> 0%
where the time goes in v1:
time: 386 us; the launch traced here: 385 us
  waiting for transfers between devices  265 us (69%)
  matrix products  50.8 us (13%)
  other arithmetic  23.7 us (6%)
  blocking collectives  20.8 us (5%)
  between operations  13.4 us (3%)
  local copies, waits for them, and re-layouts  11.4 us (3%)
    all_gather x1, waiting for transfers between devices, body(): lax.all_gather(down_weight, 'seq', axis=1, tiled=True)  85.6 us
    reduce_scatter x1, waiting for transfers between devices, body(): lax.psum_scatter(partial_out.astype(jnp.bfloat16), 'tensor', scatter_dime...  73.2 us
    ppermute x3, waiting for transfers between devices, body(): lax.ppermute(ring[-1], 'tensor', [(dev, (dev + 1) % 4) for dev in range(4)])  67.9 us
    all_gather x1, waiting for transfers between devices, body(): up_value = add_single(lax.all_gather(up_weight, 'seq', axis=0, tiled=True))  35.8 us
    dot_general x1, matrix products, body(): jnp.dot(hidden, lax.all_gather(down_weight, 'seq', axis=1, tiled=True), p...  28.8 us
    psum x1, blocking collectives, body(): lax.psum(raw_logits.astype(jnp.bfloat16), 'tensor').astype(jnp.float32)  20.8 us
    dot_general x1, matrix products, add_rows(): return jnp.dot(normed, segment, preferred_element_type=jnp.float32)  14.9 us
    unnamed x31, local copies, waits for them, and re-layouts  10.4 us
  transfers between devices with their start and end apart: 7, of which 6 were waited for; matrix products, arithmetic and copies ran while one was open for 10% of the time, Pallas kernels for 0%

profile of v1, /device:TPU:0, one launch (start us, length us, event | category | flops | bytes accessed | tf_op | source)
XLA Modules:
  0.0 385.4 jit_solution(5117807169956732216)
XLA Ops:
  6.5 0.7 all-gather.4.cloned.1.call-update
  7.3 0.7 all-gather.6.cloned.1.call-update
  8.1 0.7 all-gather.8.cloned.1.call-update
  8.8 4.2 %multiply_reduce_fusion.1 = bf16[512]{0:T(512)(128)(2,1)S(1)} fusion(f32[4,512,1024]{2,1,0:T(8,128)} %param.10), kind=kLoop, calls=%fused_computation.9 | loop fusion | flops 4193792 | bytes 8389632 | tf_op jit(solution)/shard_map/reduce_sum | solution.py:37
  13.0 1.6 copy-done
  14.6 7.2 %fusion.24 = bf16[24,512]{1,0:T(8,128)(2,1)S(1)} fusion(f32[4,512,1024]{2,1,0:T(8,128)S(1)} %copy-done, f32[24,4,1024]{2,1,0:T(4,128)S(1)} %copy-done.4), kind=kOutput, calls=%fused_computation.54 | convolution fusion | flops 603992064 | bytes 8806400 | tf_op jit(solution)/shard_map/lkd,ktd->lt/dot_general | solution.py:28
  21.8 20.8 %all-reduce = (bf16[24,512]{1,0:T(8,128)(2,1)S(1)}, bf16[1,512]{1,0:T(2,128)(2,1)S(1)}) all-reduce(bf16[24,512]{1,0:T(8,128)(2,1)S(1)} %fusion.24, bf16[1,512]{1,0:T(2,128)(2,1)S(1)} %convert_element_type.47), channel_id=1, replica_groups=mesh['seq'=8,'tensor'=4] {'tensor'}, use_global_device_ids=true, to_apply=%region_0.0 | all-reduce | flops 12800 | bytes 51200 | tf_op jit(solution)/shard_map/psum | solution.py:41
  42.6 0.7 fusion.49
  43.3 2.0 fusion.42
  45.3 4.1 %multiply_reduce_fusion = bf16[512,1024]{1,0:T(8,128)(2,1)S(1)} fusion(f32[4,512,1024]{2,1,0:T(8,128)} %param.10, f32[4,512]{1,0:T(4,128)S(1)} %get-tuple-element.29), kind=kLoop, calls=%fused_computation.8 | loop fusion | flops 3670016 | bytes 9445376 | tf_op jit(solution)/shard_map/reduce_sum | solution.py:45
  49.5 23.3 %collective-permute-done = bf16[512,1024]{1,0:T(8,128)(2,1)S(1)} collective-permute-done((bf16[512,1024]{1,0:T(8,128)(2,1)S(1)}, bf16[512,1024]{1,0:T(8,128)(2,1)S(1)}, u32[]{:S(2)}, u32[]{:S(2)}) %collective-permute-start) | collective-permute-done | bytes 1048608 | tf_op jit(solution)/shard_map/ppermute | solution.py:48
  72.8 23.3 %collective-permute-done.1 = bf16[512,1024]{1,0:T(8,128)(2,1)S(1)} collective-permute-done((bf16[512,1024]{1,0:T(8,128)(2,1)S(1)}, bf16[512,1024]{1,0:T(8,128)(2,1)S(1)}, u32[]{:S(2)}, u32[]{:S(2)}) %collective-permute-start.1) | collective-permute-done | bytes 1048608 | tf_op jit(solution)/shard_map/ppermute | solution.py:48
  96.2 21.2 %collective-permute-done.2 = bf16[512,1024]{1,0:T(8,128)(2,1)} collective-permute-done((bf16[512,1024]{1,0:T(8,128)(2,1)S(1)}, bf16[512,1024]{1,0:T(8,128)(2,1)}, u32[]{:S(2)}, u32[]{:S(2)}) %collective-permute-start.2) | collective-permute-done | bytes 1048608 | tf_op jit(solution)/shard_map/ppermute | solution.py:48
  117.4 1.3 constant_dynamic-update-slice_fusion.7
  118.8 0.1 constant_dynamic-update-slice_fusion.5
  119.0 1.3 constant_dynamic-update-slice_fusion.3
  120.4 0.1 constant_dynamic-update-slice_fusion.1
  120.6 3.4 copy-done.3
  124.0 0.9 fusion
  124.9 14.9 %fusion.27 = f32[512,1792]{1,0:T(8,128)} fusion(bf16[4096,1792]{1,0:T(8,128)(2,1)} %all-gather.4.cloned.1.call-done, f32[4096]{0:T(1024)S(1)} %convert_element_type.51, f32[512]{0:T(512)S(1)} %add_rsqrt_fusion, bf16[512,8192]{1,0:T(8,128)(2,1)} %copy-done.3, s32[]{:T(128)S(6)} %select_n.14), kind=kOutput, calls=%fused_computation.55 | convolution fusion | flops 7524581376 | bytes 22562820 | tf_op jit(solution)/shard_map/dot_general | solution.py:32
  139.8 35.8 %all-gather.6.cloned.1.call-done = bf16[4096,1792]{1,0:T(8,128)(2,1)} async-done(((bf16[512,1792]{1,0:T(8,128)(2,1)}), bf16[4096,1792]{1,0:T(8,128)(2,1)}) %all-gather.6.cloned.1.call-update) | async-done | bytes 14680080 | tf_op jit(solution)/shard_map/all_gather | solution.py:64
  175.6 85.6 %all-gather.8.cloned.1.call-done = bf16[1792,4096]{1,0:T(8,128)(2,1)} async-done(((bf16[1792,512]{1,0:T(8,128)(2,1)}), bf16[1792,4096]{1,0:T(8,128)(2,1)}) %all-gather.8.cloned.1.call-update) | async-done | bytes 14680080 | tf_op jit(solution)/shard_map/all_gather | solution.py:68
  261.3 28.8 %convolution_convert_fusion = bf16[512,4096]{1,0:T(8,128)(2,1)} fusion(bf16[1792,4096]{1,0:T(8,128)(2,1)} %all-gather.8.cloned.1.call-done, f32[512,1792]{1,0:T(8,128)} %fusion.27, bf16[4096,1792]{1,0:T(8,128)(2,1)} %all-gather.6.cloned.1.call-done, f32[4096]{0:T(1024)S(1)} %convert_element_type.51, f32[512]{0:T(512)S(1)} %add_rsqrt_fusion, ...), kind=kOutput, calls=%fused_computation.10 | convolution fusion | flops 15048376320 | bytes 41437188 | tf_op jit(solution)/shard_map/dot_general | solution.py:66
  290.1 0.6 copy-done.11
  290.8 0.7 fusion.31
  291.6 2.1 while.10
  293.8 73.2 %reduce-scatter.2.cloned.1.call-done = bf16[512,1024]{1,0:T(8,128)(2,1)} async-done(((bf16[512,4096]{1,0:T(8,128)(2,1)}), bf16[512,1024]{1,0:T(8,128)(2,1)}) %reduce-scatter.2.cloned.1.call-update) | async-done | bytes 1048592 | tf_op jit(solution)/shard_map/reduce_scatter | solution.py:71
  367.0 4.7 %fusion.7 = (f32[1,512,1024]{2,1,0:T(8,128)S(1)}, f32[1,512,1024]{2,1,0:T(8,128)S(1)}) fusion(bf16[512,1024]{1,0:T(8,128)(2,1)} %reduce-scatter.2.cloned.1.call-done, f32[4,512,1024]{2,1,0:T(8,128)} %param.10, f32[512]{0:T(512)S(1)} %bitcast.105, f32[512]{0:T(512)S(1)} %bitcast.106, f32[512]{0:T(512)S(1)} %bitcast.107, f32[512]{0:T(512)S(1)} %bitcast.100, ...), kind=kLoop, calls=%fused_computation.20 | loop fusion | flops 9961472 | bytes 13651968 | tf_op jit(solution)/shard_map/stack | solution.py:80
  371.8 1.4 copy-done.1
  373.2 0.2 copy-done.2
  373.4 1.7 fusion.17
  375.1 3.7 pad_maximum_fusion
  (102 shorter events, 2.6 us)
Async XLA Ops:
  6.5 118.4 %all-gather.4.cloned.1.call-start = ((), (), s32[]{:S(2)}) async-start(), calls=%async_computation.1 | async-start | bytes 16515072 | tf_op jit(solution)/shard_map/all_gather | solution.py:63
  7.3 168.4 %all-gather.6.cloned.1.call-start = ((), (), s32[]{:S(2)}) async-start(), calls=%async_computation.2 | async-start | bytes 16515072 | tf_op jit(solution)/shard_map/all_gather | solution.py:64
  8.0 253.3 %all-gather.8.cloned.1.call-start = ((), (), s32[]{:S(2)}) async-start(), calls=%async_computation.3 | async-start | bytes 16515072 | tf_op jit(solution)/shard_map/all_gather | solution.py:68
  8.1 4.9 %copy-start.4 = (f32[24,4,1024]{2,1,0:T(4,128)S(1)}, f32[24,4,1024]{2,1,0:T(4,128)}, u32[]{:S(2)}) copy-start(f32[24,4,1024]{2,1,0:T(4,128)} %param.11) | copy-start | bytes 1179652
  8.7 358.3 %reduce-scatter.2.cloned.1.call-start = ((), (), s32[]{:S(2)}) async-start(), calls=%async_computation.4 | async-start | bytes 5242880 | tf_op jit(solution)/shard_map/reduce_scatter | solution.py:71
  8.8 5.8 %copy-start = (f32[4,512,1024]{2,1,0:T(8,128)S(1)}, f32[4,512,1024]{2,1,0:T(8,128)}, u32[]{:S(2)}) copy-start(f32[4,512,1024]{2,1,0:T(8,128)} %param.10) | copy-start | bytes 25165828
  14.6 28.0 %copy-start.9 = (f32[3]{0:T(128)S(1)}, f32[3]{0:T(128)}, u32[]{:S(2)}) copy-start(f32[3]{0:T(128)} %param.13) | copy-start | bytes 40
  14.6 28.6 %copy-start.10 = (f32[24]{0:T(128)S(1)}, f32[24]{0:T(128)}, u32[]{:S(2)}) copy-start(f32[24]{0:T(128)} %param.12) | copy-start | bytes 292
  43.3 2.0 copy-start.5
  45.3 50.8 %copy-start.8 = (bf16[4096]{0:T(1024)(128)(2,1)S(1)}, bf16[4096]{0:T(1024)(128)(2,1)}, u32[]{:S(2)}) copy-start(bf16[4096]{0:T(1024)(128)(2,1)} %param.14) | copy-start | bytes 24580
  49.4 23.4 %collective-permute-start = (bf16[512,1024]{1,0:T(8,128)(2,1)S(1)}, bf16[512,1024]{1,0:T(8,128)(2,1)S(1)}, u32[]{:S(2)}, u32[]{:S(2)}) collective-permute-start(bf16[512,1024]{1,0:T(8,128)(2,1)S(1)} %multiply_reduce_fusion), channel_id=1, source_target_pairs={{0,1},{1,2},{2,3},{3,0},{4,5},{5,6},{6,7},{7,4},{8,9},{9,10},{10,1... | collective-permute-start | bytes 3145736 | tf_op jit(solution)/shard_map/ppermute | solution.py:48
  72.8 23.3 %collective-permute-start.1 = (bf16[512,1024]{1,0:T(8,128)(2,1)S(1)}, bf16[512,1024]{1,0:T(8,128)(2,1)S(1)}, u32[]{:S(2)}, u32[]{:S(2)}) collective-permute-start(bf16[512,1024]{1,0:T(8,128)(2,1)S(1)} %collective-permute-done), channel_id=1, source_target_pairs={{0,1},{1,2},{2,3},{3,0},{4,5},{5,6},{6,7},{7,4},{8,9},{9,10},{10,1... | collective-permute-start | bytes 3145736 | tf_op jit(solution)/shard_map/ppermute | solution.py:48
  96.1 21.3 %collective-permute-start.2 = (bf16[512,1024]{1,0:T(8,128)(2,1)S(1)}, bf16[512,1024]{1,0:T(8,128)(2,1)}, u32[]{:S(2)}, u32[]{:S(2)}) collective-permute-start(bf16[512,1024]{1,0:T(8,128)(2,1)S(1)} %collective-permute-done.1), channel_id=1, source_target_pairs={{0,1},{1,2},{2,3},{3,0},{4,5},{5,6},{6,7},{7,4},{8,9},{9,10},{10,1... | collective-permute-start | bytes 3145736 | tf_op jit(solution)/shard_map/ppermute | solution.py:48
  120.6 3.4 copy-start.3
  290.0 0.7 copy-start.11
  290.0 0.8 copy-start.6
  290.0 1.5 copy-start.7
  367.0 6.1 %copy-start.1 = (f32[4,512,1024]{2,1,0:T(8,128)S(1)}, f32[4,512,1024]{2,1,0:T(8,128)}, u32[]{:S(2)}) copy-start(f32[4,512,1024]{2,1,0:T(8,128)} %param.10) | copy-start | bytes 25165828
  367.0 6.4 %copy-start.2 = (bf16[512,1024]{1,0:T(8,128)(2,1)S(1)}, bf16[512,1024]{1,0:T(8,128)(2,1)}, u32[]{:S(2)}) copy-start(bf16[512,1024]{1,0:T(8,128)(2,1)} %reduce-scatter.2.cloned.1.call-done) | copy-start | bytes 3145732
Sparse Core Ops, SparseCore 0:
  9.2 83.5 all-gather.3
  94.7 80.8 all-gather.5
  177.5 83.7 all-gather.7
  290.2 76.7 reduce-scatter.1
